TPU v7x, 32 devices: a whole 2x2x4 slice. The times are simulated.
32 devices in a mesh: heads: 4 (over y, core), batch: 8 (over z, x).
Axes of the slice: x: 2, y: 2, z: 4, core: 2. Of those that a mesh axis runs over, the one named last changes fastest.
Arguments:
- queries: bfloat16 [64, 4096], P('batch', 'heads'), may hold values from -6 to 6
- keys_new: bfloat16 [64, 4096], P('batch', 'heads'), may hold values from -6 to 6
- values_new: bfloat16 [64, 4096], P('batch', 'heads'), may hold values from -6 to 6
- out_gate: bfloat16 [64, 4096], P('batch', 'heads'), may hold values from -6 to 6
- decay_logit: float32 [64, 32], P('batch', 'heads'), may hold values from -6 to 6
- beta_logit: float32 [64, 32], P('batch', 'heads'), may hold values from -6 to 6
- decay_rate: float32 [32], P('heads'), may hold values from 0.05 to 2
- state: float32 [64, 32, 128, 128], P('batch', 'heads'), may hold values from -0.6 to 0.6
- norm_gain: float32 [128], replicated, may hold values from 0.1 to 1.9
- out_proj: bfloat16 [4096, 4096], P('heads'), may hold values from -0.09375 to 0.09375
- residual: bfloat16 [64, 4096], P('batch'), may hold values from -40 to 40, as said below
- final_gain: float32 [4096], replicated, may hold values from 0.1 to 1.9
- value_weight: float32 [4096], replicated, may hold values from -0.09375 to 0.09375
- lm_head: bfloat16 [4096, 4096], P(None, ('heads', 'batch')), may hold values from -15 to 15
- sampled: int32 [64], replicated, may hold values from 0 to 4095
Outputs:
- logprob: float32 [64], P('batch')
- value: float32 [64], P('batch')
Inputs may be any that keep to these rules, and one draw needn't show every extreme that they name: The residual stream's entries have scales that differ by row and by column (up to tenfold each), so neither rows nor columns share one magnitude.
All inputs are finite; a program needn't handle non-finite values.
Results may differ from a plain program's by a relative error of at most 0.0013.
Values may be sent and summed in bfloat16 or wider, within the bound.
A program may use at most 64 MiB of HBM per device.

v0:
```python
import jax
import jax.numpy as jnp
from jax import lax
from jax.sharding import PartitionSpec as P

epsilon = 1e-06


def joined(part, axis, combine):
    gathered = jax.tree.map(lambda a: lax.all_gather(a, axis), part)

    def take(source):
        return jax.tree.map(lambda a: lax.dynamic_index_in_dim(a, source, 0, False), gathered)

    return lax.fori_loop(
        1, lax.axis_size(axis), lambda source, state: combine(state, take(source)), take(0)
    )


def head_outputs(
    queries, keys_new, values_new, out_gate, decay_logit, beta_logit, decay_rate, state, norm_gain
):
    rows_here, heads_here = decay_logit.shape
    query_f = queries.astype(jnp.float32).reshape(rows_here, heads_here, -1)
    key_f = keys_new.astype(jnp.float32).reshape(rows_here, heads_here, -1)
    value_f = values_new.astype(jnp.float32).reshape(rows_here, heads_here, -1)
    gate_f = out_gate.astype(jnp.float32).reshape(rows_here, heads_here, -1)
    key_size = query_f.shape[2]
    query_n = query_f / jnp.sqrt(jnp.sum(query_f * query_f, axis=2, keepdims=True) + epsilon)
    query_n = query_n * key_size ** (-0.5)
    key_n = key_f / jnp.sqrt(jnp.sum(key_f * key_f, axis=2, keepdims=True) + epsilon)
    decay = jnp.exp(-decay_rate[None, :] * jax.nn.softplus(decay_logit))
    strength = jax.nn.sigmoid(beta_logit)
    state_query = jnp.einsum("bhk,bhkv->bhv", query_n, state, precision=lax.Precision.HIGHEST)
    state_key = jnp.einsum("bhk,bhkv->bhv", key_n, state, precision=lax.Precision.HIGHEST)
    intersection = jnp.sum(query_n * key_n, axis=2, keepdims=True)
    written = value_f - decay[..., None] * state_key
    output = decay[..., None] * state_query + strength[..., None] * intersection * written
    normed = output / jnp.sqrt(jnp.mean(output * output, axis=2, keepdims=True) + epsilon)
    result = normed * norm_gain * jax.nn.silu(gate_f)
    return result.reshape(rows_here, -1).astype(jnp.bfloat16)


def merge_stats(earlier, later):
    top = jnp.maximum(earlier[0], later[0])
    total = earlier[1] * jnp.exp(earlier[0] - top) + later[1] * jnp.exp(later[0] - top)
    return (top, total, earlier[2] + later[2])


def per_device(
    queries,
    keys_new,
    values_new,
    out_gate,
    decay_logit,
    beta_logit,
    decay_rate,
    state,
    norm_gain,
    out_proj,
    residual,
    final_gain,
    value_weight,
    lm_head,
    sampled,
):
    headout = head_outputs(
        queries,
        keys_new,
        values_new,
        out_gate,
        decay_logit,
        beta_logit,
        decay_rate,
        state,
        norm_gain,
    )
    partial_out = jnp.dot(headout, out_proj, preferred_element_type=jnp.float32)
    rows_own = residual.shape[0]
    attn = lax.psum(partial_out, "heads")
    hsum = residual.astype(jnp.float32) + attn
    rstd = 1.0 / jnp.sqrt(jnp.mean(hsum * hsum, axis=1) + epsilon)
    value = rstd * jnp.sum(hsum * final_gain * value_weight, axis=1)
    normed = (hsum * rstd[:, None] * final_gain).astype(jnp.bfloat16)
    logits = jnp.dot(
        lax.all_gather(normed, "batch", axis=0, tiled=True),
        lm_head,
        preferred_element_type=jnp.float32,
    )
    vocab_own = lm_head.shape[1]
    vocab_first = lax.axis_index(("heads", "batch")) * vocab_own
    local_ids = sampled - vocab_first
    columns = lax.broadcasted_iota(jnp.int32, logits.shape, 1)
    chosen = jnp.sum(jnp.where(columns == local_ids[:, None], logits, 0.0), axis=1)
    local_top = jnp.max(logits, axis=1)
    local_total = jnp.sum(jnp.exp(logits - local_top[:, None]), axis=1)
    top, total, chosen_all = joined(
        (local_top, local_total, chosen), ("heads", "batch"), merge_stats
    )
    every_logprob = chosen_all - (top + jnp.log(total))
    logprob = lax.dynamic_slice_in_dim(
        every_logprob, lax.axis_index("batch") * rows_own, rows_own, 0
    )
    return (logprob, value)


def solution(mesh):
    placed = (
        P("batch", "heads"),
        P("batch", "heads"),
        P("batch", "heads"),
        P("batch", "heads"),
        P("batch", "heads"),
        P("batch", "heads"),
        P("heads"),
        P("batch", "heads", None, None),
        P(),
        P("heads", None),
        P("batch", None),
        P(),
        P(),
        P(None, ("heads", "batch")),
        P(),
    )
    return jax.shard_map(
        per_device, mesh=mesh, in_specs=placed, out_specs=(P("batch"), P("batch")), check_vma=False
    )
```

profile of v0, /device:TPU:0, one launch (start us, length us, event | category | flops | bytes accessed | tf_op | source)
XLA Modules:
  0.0 143.0 jit_solution(5027682328408560421)
XLA Ops:
  7.2 0.0 copy-start
  7.2 0.0 all-reduce.6.cloned.1.call-start
  7.2 0.0 copy-start.1
  7.2 1.0 fusion.7
  8.2 1.1 fusion.9
  9.3 0.9 fusion.22
  10.2 0.0 copy-start.7
  10.3 0.0 copy-start.10
  10.3 0.0 copy-start.8
  10.3 0.0 copy-start.3
  10.3 0.0 copy-start.5
  10.3 0.0 copy-start.9
  10.3 5.3 %fusion.16 = f32[8,8,1,128]{3,2,1,0:T(1,128)S(1)} fusion(f32[8,8,128,128]{3,2,1,0:T(8,128)} %param.24, f32[8,8,128,1]{2,0,1,3:T(8,128)S(1)} %get-tuple-element.209), kind=kOutput, calls=%fused_computation.32 | convolution fusion | flops 12582912 | bytes 4259840 | tf_op jit(solution)/shard_map/bhk,bhkv->bhv/dot_general | solution.py:35
  15.6 0.0 copy-done.1
  15.6 3.7 %fusion.18 = f32[8,8,1,128]{3,2,1,0:T(1,128)S(1)} fusion(f32[8,8,128,128]{3,2,1,0:T(8,128)S(1)} %copy-done.1, f32[8,8,128,1]{2,0,1,3:T(8,128)S(1)} %get-tuple-element.207), kind=kOutput, calls=%fused_computation.34 | convolution fusion | flops 12582912 | bytes 4259840 | tf_op jit(solution)/shard_map/bhk,bhkv->bhv/dot_general | solution.py:34
  19.3 0.0 copy-done.7
  19.3 0.1 copy.20
  19.4 0.0 copy-done.10
  19.4 0.0 copy-done.8
  19.4 0.1 copy.19
  19.5 0.0 copy-done.3
  19.5 0.2 multiply_reduce_fusion.2
  19.7 0.0 copy-done.5
  19.7 0.0 copy-done.9
  19.7 0.0 copy-start.11
  19.7 0.0 copy-start.2
  19.7 0.0 copy-start.4
  19.7 0.0 copy-start.6
  19.7 5.3 %fusion.23 = f32[8,4096]{1,0:T(8,128)} fusion(bf16[1024,4096]{1,0:T(8,128)(2,1)} %param.26, bf16[8,1024]{1,0:T(8,128)(2,1)S(1)} %copy-done.5, f32[128]{0:T(128)S(1)} %copy-done.9, f32[8,8]{0,1:T(8,128)S(1)} %add_sqrt_fusion, f32[8,8,1,128]{3,2,1,0:T(1,128)S(1)} %fusion.16, f32[8,8,1,128]{3,2,1,0:T(1,128)S(1)} %fusion.18, bf16[8,1024]{1,0:T(8,128)(2,1)S(1)} %copy-done.3, ...), kind=kOutput, calls=%fused_computation.44 | convolution fusion | flops 67231744 | bytes 8619264 | tf_op jit(solution)/shard_map/dot_general | solution.py:78
  25.0 0.0 all-reduce.6.cloned.1.call-update
  25.1 0.0 copy-done.11
  25.1 34.6 %all-reduce.6.cloned.1.call-done = f32[8,4096]{1,0:T(8,128)} async-done(((f32[8,4096]{1,0:T(8,128)}), f32[8,4096]{1,0:T(8,128)}) %all-reduce.6.cloned.1.call-update) | async-done | bytes 131088 | tf_op jit(solution)/shard_map/psum | solution.py:80
  59.7 0.0 copy-done.2
  59.7 0.0 copy-done.4
  59.7 0.0 copy-done.6
  59.7 1.1 multiply_reduce_fusion
  60.8 0.5 fusion.32
  61.4 1.0 multiply_convert_fusion
  62.4 31.4 %all_gather.21 = bf16[64,4096]{1,0:T(8,128)(2,1)S(1)} all-gather(bf16[8,4096]{1,0:T(8,128)(2,1)S(1)} %multiply_convert_fusion), channel_id=1, replica_groups=mesh['heads'=4,'batch'=8] {'batch'}, dimensions={0}, use_global_device_ids=true | all-gather | bytes 589824 | tf_op jit(solution)/shard_map/all_gather | solution.py:86
  93.7 0.0 copy-done
  93.7 0.4 fusion.35
  94.2 0.2 select_reduce_fusion
  94.4 0.3 dynamic-update-slice
  94.7 0.3 dynamic-update-slice.2
  94.9 0.3 dynamic-update-slice.1
  95.2 38.7 %all-reduce.3 = (f32[2048]{0:T(1024)S(1)}, f32[2048]{0:T(1024)S(1)}, f32[2048]{0:T(1024)S(1)}) all-reduce(f32[2048]{0:T(1024)S(1)} %dynamic-update-slice, f32[2048]{0:T(1024)S(1)} %dynamic-update-slice.1, f32[2048]{0:T(1024)S(1)} %dynamic-update-slice.2), channel_id=2, replica_groups=mesh['heads'=4,'batch'=8] {'heads','batch'}, use_global_device_ids=true, to_apply=%add | all-reduce | flops 6144 | bytes 49152
  133.8 0.1 reshape.81
  133.9 0.1 reshape.82
  134.0 0.1 reshape.83
  134.1 1.4 %while.19 = (s32[]{:T(128)}, f32[64]{0:T(128)S(1)}, f32[64]{0:T(128)S(1)}, f32[64]{0:T(128)S(1)}, f32[32,64]{1,0:T(8,128)S(1)}, /*index=5*/f32[32,64]{1,0:T(8,12...) while((s32[]{:T(128)}, f32[64]{0:T(128)S(1)}, f32[64]{0:T(128)S(1)}, f32[64]{0:T(128)S(1)}, ...), condition=%wide.region_10.11_spmd, body=%wide.region_9.10_spmd.sunk | while | flops 453 | bytes 2451 | solution.py:15
  135.5 0.6 dynamic_slice.46
  (44 shorter events, 0.9 us)
Async XLA Ops:
  7.2 86.6 %copy-start = (bf16[4096,128]{1,0:T(8,128)(2,1)S(1)}, bf16[4096,128]{1,0:T(8,128)(2,1)}, u32[]{:S(2)}) copy-start(bf16[4096,128]{1,0:T(8,128)(2,1)} %param.30) | copy-start | bytes 3145732
  7.2 52.6 %all-reduce.6.cloned.1.call-start = ((), (), s32[]{:S(2)}) async-start(), calls=%async_computation | async-start | bytes 262144 | tf_op jit(solution)/shard_map/psum | solution.py:80
  7.2 8.4 %copy-start.1 = (f32[8,8,128,128]{3,2,1,0:T(8,128)S(1)}, f32[8,8,128,128]{3,2,1,0:T(8,128)}, u32[]{:S(2)}) copy-start(f32[8,8,128,128]{3,2,1,0:T(8,128)} %param.24) | copy-start | bytes 12582916
  10.2 9.1 %copy-start.7 = (f32[8,8]{1,0:T(8,128)S(1)}, f32[8,8]{1,0:T(8,128)}, u32[]{:S(2)}) copy-start(f32[8,8]{1,0:T(8,128)} %param.22) | copy-start | bytes 772
  10.3 9.1 %copy-start.10 = (f32[8]{0:T(128)S(1)}, f32[8]{0:T(128)}, u32[]{:S(2)}) copy-start(f32[8]{0:T(128)} %param.23) | copy-start | bytes 100
  10.3 9.1 %copy-start.8 = (f32[8,8]{1,0:T(8,128)S(1)}, f32[8,8]{1,0:T(8,128)}, u32[]{:S(2)}) copy-start(f32[8,8]{1,0:T(8,128)} %param.21) | copy-start | bytes 772
  10.3 9.2 %copy-start.3 = (bf16[8,1024]{1,0:T(8,128)(2,1)S(1)}, bf16[8,1024]{1,0:T(8,128)(2,1)}, u32[]{:S(2)}) copy-start(bf16[8,1024]{1,0:T(8,128)(2,1)} %param.19) | copy-start | bytes 49156
  10.3 9.4 %copy-start.5 = (bf16[8,1024]{1,0:T(8,128)(2,1)S(1)}, bf16[8,1024]{1,0:T(8,128)(2,1)}, u32[]{:S(2)}) copy-start(bf16[8,1024]{1,0:T(8,128)(2,1)} %param.20) | copy-start | bytes 49156
  10.3 9.4 %copy-start.9 = (f32[128]{0:T(128)S(1)}, f32[128]{0:T(128)}, u32[]{:S(2)}) copy-start(f32[128]{0:T(128)} %param.25) | copy-start | bytes 1540
  19.7 5.4 %copy-start.11 = (s32[64]{0:T(128)S(1)}, s32[64]{0:T(128)}, u32[]{:S(2)}) copy-start(s32[64]{0:T(128)} %param.31) | copy-start | bytes 772
  19.7 40.0 %copy-start.2 = (bf16[8,4096]{1,0:T(8,128)(2,1)S(1)}, bf16[8,4096]{1,0:T(8,128)(2,1)}, u32[]{:S(2)}) copy-start(bf16[8,4096]{1,0:T(8,128)(2,1)} %param.27) | copy-start | bytes 196612
  19.7 40.0 %copy-start.4 = (f32[4096]{0:T(1024)S(1)}, f32[4096]{0:T(1024)}, u32[]{:S(2)}) copy-start(f32[4096]{0:T(1024)} %param.28) | copy-start | bytes 49156
  19.7 40.0 %copy-start.6 = (f32[4096]{0:T(1024)S(1)}, f32[4096]{0:T(1024)}, u32[]{:S(2)}) copy-start(f32[4096]{0:T(1024)} %param.29) | copy-start | bytes 49156
Sparse Core Ops, SparseCore 0:
  25.2 34.4 all-reduce.5
where the time goes:
time: 144 us; the launch traced here: 143 us
  blocking collectives  70.1 us (49%)
  waiting for transfers between devices  34.6 us (24%)
  matrix products  14.7 us (10%)
  between operations  14.2 us (10%)
  other arithmetic  6.89 us (5%)
  local copies, waits for them, and re-layouts  1.82 us (1%)
    unnamed x1, blocking collectives  38.7 us
    psum x1, waiting for transfers between devices, per_device(): attn = lax.psum(partial_out, 'heads')  34.6 us
    all_gather x1, blocking collectives, per_device(): lax.all_gather(normed, 'batch', axis=0, tiled=True)  31.4 us
    dot_general x1, matrix products, head_outputs(): jnp.einsum('bhk,bhkv->bhv', key_n, state, precision=lax.Precision.HIGHEST)  5.31 us
    dot_general x1, matrix products, per_device(): partial_out = jnp.dot(headout, out_proj, preferred_element_type=jnp.float32)  5.31 us
    dot_general x1, matrix products, head_outputs(): jnp.einsum('bhk,bhkv->bhv', query_n, state, precision=lax.Precision.HIGHEST)  3.66 us
  transfers between devices with their start and end apart: 1, of which 1 were waited for; matrix products, arithmetic and copies ran while one was open for 0% of the time, Pallas kernels for 0%

commit v1 on v0

--- a/solution.py
+++ b/solution.py
@@ -77,7 +77,7 @@
     )
     partial_out = jnp.dot(headout, out_proj, preferred_element_type=jnp.float32)
     rows_own = residual.shape[0]
-    attn = lax.psum(partial_out, "heads")
+    attn = jnp.sum(lax.all_gather(partial_out, "heads"), axis=0)
     hsum = residual.astype(jnp.float32) + attn
     rstd = 1.0 / jnp.sqrt(jnp.mean(hsum * hsum, axis=1) + epsilon)
     value = rstd * jnp.sum(hsum * final_gain * value_weight, axis=1)

time: 144 us -> 103 us (0.72)
  waiting for transfers between devices: 34.6 us -> 0 us
  between operations: 14.2 us -> 0.89 us
  blocking collectives: 70.1 us -> 79.7 us
  other arithmetic: 6.89 us -> 5.12 us
    psum x1 -> x0, waiting for transfers between devices: 34.6 us -> none  [per_device(): attn = lax.psum(partial_out, 'heads')]
    all_gather x0 -> x1, blocking collectives: none -> 8.67 us  [per_device(): attn = jnp.sum(lax.all_gather(partial_out, 'heads'), axis=0)]
  transfers between devices with their start and end apart: 1 -> 0, of which waited for: 1 -> 0; matrix products, arithmetic and copies ran while one was open for 0% -> 0% of each run, Pallas kernels for 0% -> 0%
where the time goes in v1:
time: 103 us; the launch traced here: 102 us
  blocking collectives  79.7 us (77%)
  matrix products  14 us (14%)
  other arithmetic  5.12 us (5%)
  local copies, waits for them, and re-layouts  1.82 us (2%)
    unnamed x1, blocking collectives  39.2 us
    all_gather x1, blocking collectives, per_device(): lax.all_gather(normed, 'batch', axis=0, tiled=True)  31.9 us
    all_gather x1, blocking collectives, per_device(): attn = jnp.sum(lax.all_gather(partial_out, 'heads'), axis=0)  8.67 us
    dot_general x1, matrix products, head_outputs(): jnp.einsum('bhk,bhkv->bhv', key_n, state, precision=lax.Precision.HIGHEST)  5.31 us
    dot_general x1, matrix products, per_device(): partial_out = jnp.dot(headout, out_proj, preferred_element_type=jnp.float32)  4.63 us
    dot_general x1, matrix products, head_outputs(): jnp.einsum('bhk,bhkv->bhv', query_n, state, precision=lax.Precision.HIGHEST)  3.66 us

profile of v1, /device:TPU:0, one launch (start us, length us, event | category | flops | bytes accessed | tf_op | source)
XLA Modules:
  0.0 102.1 jit_solution(3245902324087259836)
XLA Ops:
  0.6 0.0 copy-start
  0.6 0.0 copy-start.1
  0.7 1.0 fusion.7
  1.6 1.1 %fusion.9 = f32[8,8]{0,1:T(8,128)S(1)} fusion(bf16[8,1024]{1,0:T(8,128)(2,1)} %param.18), kind=kLoop, calls=%fused_computation.23 | loop fusion | flops 24512 | bytes 16640 | tf_op jit(solution)/shard_map/reduce_sum | solution.py:31
  2.8 0.9 fusion.22
  3.7 0.0 copy-start.7
  3.7 0.0 copy-start.10
  3.7 0.0 copy-start.8
  3.7 0.0 copy-start.3
  3.7 0.0 copy-start.5
  3.7 0.0 copy-start.9
  3.7 5.3 %fusion.16 = f32[8,8,1,128]{3,2,1,0:T(1,128)S(1)} fusion(f32[8,8,128,128]{3,2,1,0:T(8,128)} %param.24, f32[8,8,128,1]{2,0,1,3:T(8,128)S(1)} %get-tuple-element.209), kind=kOutput, calls=%fused_computation.33 | convolution fusion | flops 12582912 | bytes 4259840 | tf_op jit(solution)/shard_map/bhk,bhkv->bhv/dot_general | solution.py:35
  9.1 0.0 copy-done.1
  9.1 3.7 %fusion.18 = f32[8,8,1,128]{3,2,1,0:T(1,128)S(1)} fusion(f32[8,8,128,128]{3,2,1,0:T(8,128)S(1)} %copy-done.1, f32[8,8,128,1]{2,0,1,3:T(8,128)S(1)} %get-tuple-element.207), kind=kOutput, calls=%fused_computation.35 | convolution fusion | flops 12582912 | bytes 4259840 | tf_op jit(solution)/shard_map/bhk,bhkv->bhv/dot_general | solution.py:34
  12.7 0.0 copy-done.7
  12.7 0.1 copy.20
  12.8 0.0 copy-done.10
  12.8 0.0 copy-done.8
  12.8 0.1 copy.19
  12.9 0.0 copy-done.3
  12.9 0.2 multiply_reduce_fusion.2
  13.1 0.0 copy-done.5
  13.1 0.0 copy-done.9
  13.1 0.0 copy-start.2
  13.1 0.0 copy-start.4
  13.1 0.0 copy-start.6
  13.2 0.0 copy-start.11
  13.2 4.6 %fusion.23 = f32[8,4096]{1,0:T(8,128)S(1)} fusion(bf16[1024,4096]{1,0:T(8,128)(2,1)} %param.26, bf16[8,1024]{1,0:T(8,128)(2,1)S(1)} %copy-done.5, f32[128]{0:T(128)S(1)} %copy-done.9, f32[8,8]{0,1:T(8,128)S(1)} %add_sqrt_fusion, f32[8,8,1,128]{3,2,1,0:T(1,128)S(1)} %fusion.16, f32[8,8,1,128]{3,2,1,0:T(1,128)S(1)} %fusion.18, ...), kind=kOutput, calls=%fused_computation.45 | convolution fusion | flops 67231744 | bytes 8619264 | tf_op jit(solution)/shard_map/dot_general | solution.py:78
  17.8 8.7 %all-gather = f32[32,4096]{1,0:T(8,128)S(1)} all-gather(f32[8,4096]{1,0:T(8,128)S(1)} %fusion.23), channel_id=2, replica_groups=mesh['heads'=4,'batch'=8] {'heads'}, dimensions={0}, use_global_device_ids=true | all-gather | bytes 655360 | tf_op jit(solution)/shard_map/all_gather | solution.py:80
  26.5 0.0 copy-done.2
  26.5 0.0 copy-done.4
  26.5 0.0 copy-done.6
  26.5 0.2 multiply_reduce_fusion
  26.7 0.5 fusion.32
  27.3 0.1 multiply_convert_fusion
  27.3 31.9 %all_gather.29 = bf16[64,4096]{1,0:T(8,128)(2,1)S(1)} all-gather(bf16[8,4096]{1,0:T(8,128)(2,1)S(1)} %multiply_convert_fusion), channel_id=1, replica_groups=mesh['heads'=4,'batch'=8] {'batch'}, dimensions={0}, use_global_device_ids=true | all-gather | bytes 589824 | tf_op jit(solution)/shard_map/all_gather | solution.py:86
  59.2 0.0 copy-done
  59.2 0.4 fusion.35
  59.6 0.0 copy-done.11
  59.7 0.2 select_reduce_fusion
  59.9 0.3 dynamic-update-slice.2
  60.1 0.3 dynamic-update-slice.1
  60.4 0.3 dynamic-update-slice
  60.7 39.2 %all-reduce.3 = (f32[2048]{0:T(1024)S(1)}, f32[2048]{0:T(1024)S(1)}, f32[2048]{0:T(1024)S(1)}) all-reduce(f32[2048]{0:T(1024)S(1)} %dynamic-update-slice, f32[2048]{0:T(1024)S(1)} %dynamic-update-slice.1, f32[2048]{0:T(1024)S(1)} %dynamic-update-slice.2), channel_id=3, replica_groups=mesh['heads'=4,'batch'=8] {'heads','batch'}, use_global_device_ids=true, to_apply=%add | all-reduce | flops 6144 | bytes 49152
  99.8 0.1 reshape.82
  99.9 0.1 reshape.83
  100.0 0.1 reshape.84
  100.1 1.4 %while.19 = (s32[]{:T(128)}, f32[64]{0:T(128)S(1)}, f32[64]{0:T(128)S(1)}, f32[64]{0:T(128)S(1)}, f32[32,64]{1,0:T(8,128)S(1)}, /*index=5*/f32[32,64]{1,0:T(8,12...) while((s32[]{:T(128)}, f32[64]{0:T(128)S(1)}, f32[64]{0:T(128)S(1)}, f32[64]{0:T(128)S(1)}, ...), condition=%wide.region_10.11_spmd, body=%wide.region_9.10_spmd.sunk | while | flops 453 | bytes 2451 | solution.py:15
  101.5 0.6 dynamic_slice.46
  (45 shorter events, 1.0 us)
Async XLA Ops:
  0.6 58.6 %copy-start = (bf16[4096,128]{1,0:T(8,128)(2,1)S(1)}, bf16[4096,128]{1,0:T(8,128)(2,1)}, u32[]{:S(2)}) copy-start(bf16[4096,128]{1,0:T(8,128)(2,1)} %param.30) | copy-start | bytes 3145732
  0.6 8.4 %copy-start.1 = (f32[8,8,128,128]{3,2,1,0:T(8,128)S(1)}, f32[8,8,128,128]{3,2,1,0:T(8,128)}, u32[]{:S(2)}) copy-start(f32[8,8,128,128]{3,2,1,0:T(8,128)} %param.24) | copy-start | bytes 12582916
  3.7 9.1 %copy-start.7 = (f32[8,8]{1,0:T(8,128)S(1)}, f32[8,8]{1,0:T(8,128)}, u32[]{:S(2)}) copy-start(f32[8,8]{1,0:T(8,128)} %param.22) | copy-start | bytes 772
  3.7 9.1 %copy-start.10 = (f32[8]{0:T(128)S(1)}, f32[8]{0:T(128)}, u32[]{:S(2)}) copy-start(f32[8]{0:T(128)} %param.23) | copy-start | bytes 100
  3.7 9.1 %copy-start.8 = (f32[8,8]{1,0:T(8,128)S(1)}, f32[8,8]{1,0:T(8,128)}, u32[]{:S(2)}) copy-start(f32[8,8]{1,0:T(8,128)} %param.21) | copy-start | bytes 772
  3.7 9.2 %copy-start.3 = (bf16[8,1024]{1,0:T(8,128)(2,1)S(1)}, bf16[8,1024]{1,0:T(8,128)(2,1)}, u32[]{:S(2)}) copy-start(bf16[8,1024]{1,0:T(8,128)(2,1)} %param.19) | copy-start | bytes 49156
  3.7 9.4 %copy-start.5 = (bf16[8,1024]{1,0:T(8,128)(2,1)S(1)}, bf16[8,1024]{1,0:T(8,128)(2,1)}, u32[]{:S(2)}) copy-start(bf16[8,1024]{1,0:T(8,128)(2,1)} %param.20) | copy-start | bytes 49156
  3.7 9.4 %copy-start.9 = (f32[128]{0:T(128)S(1)}, f32[128]{0:T(128)}, u32[]{:S(2)}) copy-start(f32[128]{0:T(128)} %param.25) | copy-start | bytes 1540
  13.1 13.4 %copy-start.2 = (bf16[8,4096]{1,0:T(8,128)(2,1)S(1)}, bf16[8,4096]{1,0:T(8,128)(2,1)}, u32[]{:S(2)}) copy-start(bf16[8,4096]{1,0:T(8,128)(2,1)} %param.27) | copy-start | bytes 196612
  13.1 13.4 %copy-start.4 = (f32[4096]{0:T(1024)S(1)}, f32[4096]{0:T(1024)}, u32[]{:S(2)}) copy-start(f32[4096]{0:T(1024)} %param.28) | copy-start | bytes 49156
  13.1 13.4 %copy-start.6 = (f32[4096]{0:T(1024)S(1)}, f32[4096]{0:T(1024)}, u32[]{:S(2)}) copy-start(f32[4096]{0:T(1024)} %param.29) | copy-start | bytes 49156
  13.2 46.5 %copy-start.11 = (s32[64]{0:T(128)S(1)}, s32[64]{0:T(128)}, u32[]{:S(2)}) copy-start(s32[64]{0:T(128)} %param.31) | copy-start | bytes 772
